TPU v7x, 32 devices: a whole 2x2x4 slice. The times are simulated.
32 devices in a mesh: wide: 16 (over z, y, x), narrow: 2 (over core).
Axes of the slice: x: 2, y: 2, z: 4, core: 2. Of those that a mesh axis runs over, the one named last changes fastest.
Arguments:
- node_latent: bfloat16 [4096, 512], P(('wide', 'narrow')), may hold values from -6 to 6
- edge_latent: bfloat16 [16384, 512], P(('wide', 'narrow')), may hold values from -6 to 6
- node_cotangent: bfloat16 [4096, 512], P(('wide', 'narrow')), may hold values from -6 to 6
- w_first: bfloat16 [1536, 512], replicated, may hold values from -2 to 2
- bias_first: bfloat16 [512], replicated, may hold values from -4 to 4
- w_second: bfloat16 [512, 512], replicated, may hold values from -2 to 2
- bias_second: bfloat16 [512], replicated, may hold values from -4 to 4
- norm_gain: bfloat16 [512], replicated, may hold values from 0.099609375 to 1.8984375
- send_map: int32 [32, 4, 64], P(('wide', 'narrow')), may hold values from -1 to 127, as said below
- edge_sender: int32 [16384], P(('wide', 'narrow')), may hold values from 0 to 383, as said below
- edge_receiver: int32 [16384], P(('wide', 'narrow')), may hold values from 0 to 127
Outputs:
- node_grad: bfloat16 [4096, 512], P(('wide', 'narrow'))
- edge_grad: bfloat16 [16384, 512], P(('wide', 'narrow'))
- first_update: float32 [1536, 512], P('wide')
- second_update: float32 [512, 512], P('wide')
Inputs may be any that keep to these rules, and one draw needn't show every extreme that they name: `send_map`: -1 marks an unused slot; in each row the used slots come first, at most 64, about a third of them on average; in every draw some partition uses all 64 slots toward a wide neighbour; partitions at narrow index 0 send nothing toward block 3 of a lower neighbour and those at the last narrow index nothing toward a higher one. `edge_sender`: a value below 128 is a local node; 128 + k * 64 + s names slot s of received block k, and only slots that the sending partition uses are named.
All inputs are finite; a program needn't handle non-finite values.
Results may differ from a plain program's by a relative error of at most 0.0085.
Values may be sent and summed in bfloat16 or wider, within the bound.
No kernel may reach another device: no remote copies, remote signals or barrier semaphores. Data moves between devices by JAX's collectives and lax.ppermute only.
A program may use at most 64 MiB of HBM per device.

v0:
```python
import math
import jax
import jax.numpy as jnp
from jax import lax
from jax.sharding import PartitionSpec as P


def shifted(value, axis, steps):
    count = lax.axis_size(axis)
    pairs = [(source, (source + steps) % count) for source in range(count)]
    return lax.ppermute(value, axis, pairs)


def shifted_2(block, axis, distance):
    devices = range(lax.axis_size(axis))
    route = [(i - distance, i) for i in devices if i - distance in devices]
    return lax.ppermute(block, axis, route)


def neighbours(blocks, direction):
    higher = shifted(blocks[0], "wide", direction)
    lower = shifted(blocks[1], "wide", -direction)
    up_side = shifted_2(blocks[2], "narrow", direction)
    down_side = shifted_2(blocks[3], "narrow", -direction)
    return jnp.stack([higher, lower, up_side, down_side], 0)


def norm_parts(second_pre):
    mean_value = jnp.mean(second_pre, -1, keepdims=True)
    centered = second_pre - mean_value
    variance = jnp.mean(centered * centered, -1, keepdims=True)
    inv_std = lax.rsqrt(variance + 1e-05)
    return (centered * inv_std, inv_std)


def clip_share(grad_share, grad_sq, weight_sq, fan_rows):
    unit_ratio = jnp.sqrt((grad_sq + 1e-06) / (weight_sq + 1e-06))
    mean_ratio = jnp.mean(unit_ratio)
    factor = jnp.minimum(
        1.0 / (mean_ratio * jnp.sqrt(weight_sq + 1e-06)), 1.0 / jnp.sqrt(grad_sq + 1e-06)
    )
    return grad_share * factor * math.sqrt(fan_rows)


def edge_contract(hot_table, values):
    return lax.dot_general(
        hot_table,
        values,
        (((0,), (0,)), ((), ())),
        precision=lax.Precision.HIGHEST,
        preferred_element_type=jnp.float32,
    )


def per_device(
    node_latent,
    edge_latent,
    node_cotangent,
    w_first,
    bias_first,
    w_second,
    bias_second,
    norm_gain,
    send_map,
    edge_sender,
    edge_receiver,
):
    node_count, feature_width = node_latent.shape
    halo_slots = send_map.shape[2]
    table_rows = node_count + 4 * halo_slots
    send_hot = (send_map[0][:, :, None] == jnp.arange(node_count, dtype=jnp.int32)).astype(
        jnp.bfloat16
    )
    outgoing = jnp.einsum(
        "khn,nd->khd", send_hot, node_latent, preferred_element_type=jnp.float32
    ).astype(jnp.bfloat16)
    received = neighbours(outgoing, 1)
    node_table = jnp.concatenate([node_latent, received.reshape(4 * halo_slots, feature_width)], 0)
    sender_hot = (edge_sender[:, None] == jnp.arange(table_rows, dtype=jnp.int32)).astype(
        jnp.bfloat16
    )
    receiver_hot = (edge_receiver[:, None] == jnp.arange(node_count, dtype=jnp.int32)).astype(
        jnp.bfloat16
    )
    sender_rows = jnp.dot(sender_hot, node_table, preferred_element_type=jnp.float32).astype(
        jnp.bfloat16
    )
    receiver_rows = jnp.dot(receiver_hot, node_latent, preferred_element_type=jnp.float32).astype(
        jnp.bfloat16
    )
    inputs = jnp.concatenate([edge_latent, sender_rows, receiver_rows], 1)
    preact = jnp.dot(inputs, w_first, preferred_element_type=jnp.float32) + bias_first.astype(
        jnp.float32
    )
    activation = jax.nn.silu(preact).astype(jnp.bfloat16)
    second_pre = jnp.dot(
        activation, w_second, preferred_element_type=jnp.float32
    ) + bias_second.astype(jnp.float32)
    normalized, inv_std = norm_parts(second_pre)
    upstream = jnp.dot(receiver_hot, node_cotangent, preferred_element_type=jnp.float32)
    scaled = upstream * norm_gain.astype(jnp.float32)
    norm_back = (
        inv_std
        * (
            scaled
            - jnp.mean(scaled, -1, keepdims=True)
            - normalized * jnp.mean(scaled * normalized, -1, keepdims=True)
        )
    ).astype(jnp.bfloat16)
    second_grad = lax.dot_general(
        activation, norm_back, (((0,), (0,)), ((), ())), preferred_element_type=jnp.float32
    )
    sigmoid_pre = jax.nn.sigmoid(preact)
    pre_back = (
        jnp.dot(norm_back, w_second.T, preferred_element_type=jnp.float32)
        * sigmoid_pre
        * (1.0 + preact * (1.0 - sigmoid_pre))
    ).astype(jnp.bfloat16)
    first_grad = lax.dot_general(
        inputs, pre_back, (((0,), (0,)), ((), ())), preferred_element_type=jnp.float32
    )
    input_back = jnp.dot(pre_back, w_first.T, preferred_element_type=jnp.float32)
    edge_grad = (upstream + input_back[:, :feature_width]).astype(jnp.bfloat16)
    table_grad = edge_contract(
        sender_hot.astype(jnp.float32), input_back[:, feature_width : 2 * feature_width]
    )
    receiver_grad = edge_contract(
        receiver_hot.astype(jnp.float32), input_back[:, 2 * feature_width :]
    )
    halo_grad = table_grad[node_count:].reshape(4, halo_slots, feature_width).astype(jnp.bfloat16)
    returned = neighbours(halo_grad, -1)
    back = jnp.einsum("khn,khd->nd", send_hot, returned, preferred_element_type=jnp.float32)
    node_grad = (
        node_cotangent.astype(jnp.float32) + table_grad[:node_count] + receiver_grad + back
    ).astype(jnp.bfloat16)
    wide_count = lax.axis_size("wide")
    first_rows = w_first.shape[0] // wide_count
    second_rows = w_second.shape[0] // wide_count
    first_weight_sq = jnp.sum(jnp.square(w_first.astype(jnp.float32)), 0)
    second_weight_sq = jnp.sum(jnp.square(w_second.astype(jnp.float32)), 0)
    first_total, second_total = lax.psum((first_grad, second_grad), ("wide", "narrow"))
    position = lax.axis_index("wide")
    first_share = lax.dynamic_slice_in_dim(first_total, position * first_rows, first_rows, 0)
    second_share = lax.dynamic_slice_in_dim(second_total, position * second_rows, second_rows, 0)
    first_grad_sq = jnp.sum(first_total * first_total, 0)
    second_grad_sq = jnp.sum(second_total * second_total, 0)
    first_update = clip_share(first_share, first_grad_sq, first_weight_sq, w_first.shape[0])
    second_update = clip_share(second_share, second_grad_sq, second_weight_sq, w_second.shape[0])
    return (node_grad, edge_grad, first_update, second_update)


def solution(mesh):
    return jax.shard_map(
        per_device,
        mesh=mesh,
        in_specs=(
            P(("wide", "narrow"), None),
            P(("wide", "narrow"), None),
            P(("wide", "narrow"), None),
            P(),
            P(),
            P(),
            P(),
            P(),
            P(("wide", "narrow"), None, None),
            P(("wide", "narrow")),
            P(("wide", "narrow")),
        ),
        out_specs=(
            P(("wide", "narrow"), None),
            P(("wide", "narrow"), None),
            P("wide", None),
            P("wide", None),
        ),
        check_vma=False,
    )
```

profile of v0, /device:TPU:0, one launch (start us, length us, event | category | flops | bytes accessed | tf_op | source)
XLA Modules:
  0.0 192.4 jit_solution(14532633733271048976)
XLA Ops:
  7.2 0.0 copy-start.4
  7.2 0.0 copy-start.8
  7.2 0.0 copy-start.1
  7.2 0.0 all-reduce.3.cloned.1.call-start
  7.2 1.3 convolution_convert_fusion.2
  8.6 1.3 collective-permute-start.3
  9.9 3.0 %collective-permute-start.2 = (bf16[64,512]{1,0:T(8,128)(2,1)S(1)}, bf16[64,512]{1,0:T(8,128)(2,1)S(1)}, u32[]{:S(2)}, u32[]{:S(2)}) collective-permute-start(bf16[64,512]{1,0:T(8,128)(2,1)S(1)} %get-tuple-element.18), channel_id=1, source_target_pairs={{0,1},{2,3},{4,5},{6,7},{8,9},{10,11},{12,13},{14,15},{16,17},{18,... | collective-permute-start | bytes 196616 | tf_op jit(solution)/shard_map/ppermute | solution.py:17
  12.9 7.0 %collective-permute-start.1 = (bf16[64,512]{1,0:T(8,128)(2,1)S(1)}, bf16[64,512]{1,0:T(8,128)(2,1)S(1)}, u32[]{:S(2)}, u32[]{:S(2)}) collective-permute-start(bf16[64,512]{1,0:T(8,128)(2,1)S(1)} %get-tuple-element.19), channel_id=1, source_target_pairs={{0,30},{2,0},{4,2},{6,4},{8,6},{10,8},{12,10},{14,12},{16,14},{18,... | collective-permute-start | bytes 196616 | tf_op jit(solution)/shard_map/ppermute | solution.py:11
  19.9 0.0 collective-permute-start
  19.9 1.3 convolution_convert_fusion.1
  21.3 0.7 convert_element_type.56
  22.0 0.7 convert_element_type.55
  22.6 1.3 copy.15
  23.9 0.7 convert_element_type.53
  24.6 0.0 collective-permute-done.3
  24.6 0.0 collective-permute-done.2
  24.6 0.0 collective-permute-done.1
  24.6 3.2 %collective-permute-done = bf16[64,512]{1,0:T(8,128)(2,1)S(1)} collective-permute-done((bf16[64,512]{1,0:T(8,128)(2,1)S(1)}, bf16[64,512]{1,0:T(8,128)(2,1)S(1)}, u32[]{:S(2)}, u32[]{:S(2)}) %collective-permute-start) | collective-permute-done | bytes 65568 | tf_op jit(solution)/shard_map/ppermute | solution.py:11
  27.8 0.0 copy-done.4
  27.8 0.0 copy-done.8
  27.9 0.6 convolution_convert_fusion
  28.5 0.0 copy-done.1
  28.5 0.0 copy-start.5
  28.5 1.0 convolution_add_fusion.1
  29.5 0.0 copy-done.5
  29.5 0.6 fusion.33
  30.2 0.2 multiply_reduce_fusion.5
  30.4 0.1 copy-done.6
  30.4 0.0 copy-done.7
  30.4 0.5 multiply_reduce_fusion.6
  31.0 0.3 multiply_convert_fusion
  31.3 0.7 fusion.1
  31.9 0.1 copy-done
  32.0 1.5 fusion.31
  33.5 0.0 copy-done.3
  33.5 2.7 %fusion.7 = f32[1536,512]{1,0:T(8,128)} fusion(bf16[512,512]{1,0:T(8,128)(2,1)S(1)} %fusion.1, bf16[512,512]{0,1:T(8,128)(2,1)S(1)} %convolution_convert_fusion.1, bf16[512,512]{0,1:T(8,128)(2,1)S(1)} %convolution_convert_fusion, bf16[512,512]{0,1:T(8,128)(2,1)S(1)} %copy.15), kind=kOutput, calls=%fused_computation.28 | convolution fusion | flops 810024960 | bytes 5242880 | tf_op jit(solution)/shard_map/dot_general | solution.py:119
  36.2 0.0 all-reduce.3.cloned.1.call-update
  36.2 0.2 multiply_reduce_fusion.2
  36.4 0.4 multiply_reduce_fusion
  36.8 2.6 %fusion.35 = f32[512,1536]{1,0:T(8,128)S(1)} fusion(bf16[512,512]{1,0:T(8,128)(2,1)} %copy-done.3, bf16[1536,512]{1,0:T(8,128)(2,1)} %param.14), kind=kOutput, calls=%fused_computation.74 | convolution fusion | flops 805306368 | bytes 5242880 | tf_op jit(solution)/shard_map/dot_general | solution.py:122
  39.3 1.0 slice.69
  40.4 1.8 fusion.34
  42.3 1.9 collective-permute-start.7
  44.2 1.3 collective-permute-start.6
  45.5 0.1 collective-permute-start.5
  45.5 5.6 %collective-permute-start.4 = (bf16[64,512]{1,0:T(8,128)(2,1)S(1)}, bf16[64,512]{1,0:T(8,128)(2,1)}, u32[]{:S(2)}, u32[]{:S(2)}) collective-permute-start(bf16[64,512]{1,0:T(8,128)(2,1)S(1)} %get-tuple-element.12), channel_id=1, source_target_pairs={{0,30},{2,0},{4,2},{6,4},{8,6},{10,8},{12,10},{14,12},{16,14},{18,... | collective-permute-start | bytes 196616 | tf_op jit(solution)/shard_map/ppermute | solution.py:11
  51.1 2.6 %copy.18 = f32[512,512]{0,1:T(8,128)} copy(f32[512,512]{1,0:T(8,128)} %slice.69) | data formatting | bytes 2097152
  53.7 2.6 %add_convert_fusion = bf16[512,512]{0,1:T(8,128)(2,1)} fusion(f32[512,512]{0,1:T(8,128)} %copy-done, f32[512,512]{0,1:T(8,128)} %copy.18), kind=kLoop, calls=%fused_computation.20 | loop fusion | flops 524288 | bytes 2621440 | tf_op jit(solution)/shard_map/convert_element_type | solution.py:123
  56.2 2.3 %convolution_add_fusion.2 = f32[128,512]{1,0:T(8,128)} fusion(f32[512,1536]{1,0:T(8,128)S(1)} %fusion.35, f32[384,512]{1,0:T(8,128)} %get-tuple-element.24, bf16[128,512]{1,0:T(8,128)(2,1)S(1)} %copy-done.6, s32[512]{0:T(512)S(1)} %copy-done.7), kind=kOutput, calls=%fused_computation.12 | convolution fusion | flops 402915328 | bytes 1705984 | tf_op jit(solution)/shard_map/dot_general | solution.py:46
  58.5 2.0 %copy.17 = bf16[512,512]{1,0:T(8,128)(2,1)} copy(bf16[512,512]{0,1:T(8,128)(2,1)} %add_convert_fusion) | data formatting | bytes 1048576
  60.6 0.0 collective-permute-done.7
  60.6 0.0 collective-permute-done.6
  60.6 0.0 collective-permute-done.5
  60.6 0.0 collective-permute-done.4
  60.6 0.0 copy-done.9
  60.6 2.0 %fusion.3 = bf16[128,512]{1,0:T(8,128)(2,1)} fusion(f32[128,512]{1,0:T(8,128)} %convolution_add_fusion.2, bf16[1,64,512]{2,1,0:T(8,128)(2,1)} %bitcast.14, bf16[1,64,512]{2,1,0:T(8,128)(2,1)} %bitcast.13, bf16[1,64,512]{2,1,0:T(8,128)(2,1)} %bitcast.12, bf16[1,64,512]{2,1,0:T(8,128)(2,1)} %bitcast.11, s32[4,64]{1,0:T(4,128)S(1)} %bitcast.43), kind=kOutput, calls=%fused_computation.14 | convolution fusion | flops 34111488 | bytes 656384 | tf_op jit(solution)/shard_map/khn,khd->nd/dot_general | solution.py:132
  62.6 115.6 %all-reduce.3.cloned.1.call-done = (f32[1536,512]{1,0:T(8,128)}, f32[512,512]{1,0:T(8,128)}) async-done(((f32[1536,512]{1,0:T(8,128)}, f32[512,512]{1,0:T(8,128)}), (f32[1536,512]{1,0:T(8,128)}, f32[512,512]{1,0:T(8,128)})) %all-reduce.3.cloned.1.call-update) | async-done | bytes 4194320 | tf_op jit(solution)/shard_map/psum | solution.py:141
  178.3 2.3 %multiply_reduce_fusion.1 = f32[512]{0:T(512)S(1)} fusion(f32[1536,512]{1,0:T(8,128)} %get-tuple-element.10), kind=kLoop, calls=%fused_computation.1 | loop fusion | flops 1572352 | bytes 3147776 | tf_op jit(solution)/shard_map/reduce_sum | solution.py:145
  180.5 0.6 sqrt_reduce_fusion.1
  181.8 0.0 copy-done.2
  181.8 0.1 multiply_reduce_fusion.3
  182.0 0.6 sqrt_reduce_fusion
  183.2 1.6 multiply_multiply_fusion
  184.9 0.6 multiply_multiply_fusion.1
  (14 shorter events, 0.1 us)
Async XLA Ops:
  7.2 20.7 %copy-start.4 = (bf16[128,512]{1,0:T(8,128)(2,1)S(1)}, bf16[128,512]{1,0:T(8,128)(2,1)}, u32[]{:S(2)}) copy-start(bf16[128,512]{1,0:T(8,128)(2,1)} %param.11) | copy-start | bytes 393220
  7.2 20.7 %copy-start.8 = (s32[512]{0:T(512)S(1)}, s32[512]{0:T(512)}, u32[]{:S(2)}) copy-start(s32[512]{0:T(512)} %param.20) | copy-start | bytes 6148
  7.2 21.3 %copy-start.1 = (bf16[1536,512]{1,0:T(8,128)(2,1)S(1)}, bf16[1536,512]{1,0:T(8,128)(2,1)}, u32[]{:S(2)}) copy-start(bf16[1536,512]{1,0:T(8,128)(2,1)} %param.14) | copy-start | bytes 4718596
  7.2 171.1 %all-reduce.3.cloned.1.call-start = ((), (), s32[]{:S(2)}) async-start(), calls=%async_computation | async-start | bytes 8388608 | tf_op jit(solution)/shard_map/psum | solution.py:141
  8.6 16.0 %collective-permute-start.3 = (bf16[64,512]{1,0:T(8,128)(2,1)S(1)}, bf16[64,512]{1,0:T(8,128)(2,1)S(1)}, u32[]{:S(2)}, u32[]{:S(2)}) collective-permute-start(bf16[64,512]{1,0:T(8,128)(2,1)S(1)} %get-tuple-element.17), channel_id=1, source_target_pairs={{1,0},{3,2},{5,4},{7,6},{9,8},{11,10},{13,12},{15,14},{17,16},{19,... | collective-permute-start | bytes 196616 | tf_op jit(solution)/shard_map/ppermute | solution.py:17
  9.9 14.7 %collective-permute-start.2 = (bf16[64,512]{1,0:T(8,128)(2,1)S(1)}, bf16[64,512]{1,0:T(8,128)(2,1)S(1)}, u32[]{:S(2)}, u32[]{:S(2)}) collective-permute-start(bf16[64,512]{1,0:T(8,128)(2,1)S(1)} %get-tuple-element.18), channel_id=1, source_target_pairs={{0,1},{2,3},{4,5},{6,7},{8,9},{10,11},{12,13},{14,15},{16,17},{18,... | collective-permute-start | bytes 196616 | tf_op jit(solution)/shard_map/ppermute | solution.py:17
  12.9 11.7 %collective-permute-start.1 = (bf16[64,512]{1,0:T(8,128)(2,1)S(1)}, bf16[64,512]{1,0:T(8,128)(2,1)S(1)}, u32[]{:S(2)}, u32[]{:S(2)}) collective-permute-start(bf16[64,512]{1,0:T(8,128)(2,1)S(1)} %get-tuple-element.19), channel_id=1, source_target_pairs={{0,30},{2,0},{4,2},{6,4},{8,6},{10,8},{12,10},{14,12},{16,14},{18,... | collective-permute-start | bytes 196616 | tf_op jit(solution)/shard_map/ppermute | solution.py:11
  19.9 7.9 %collective-permute-start = (bf16[64,512]{1,0:T(8,128)(2,1)S(1)}, bf16[64,512]{1,0:T(8,128)(2,1)S(1)}, u32[]{:S(2)}, u32[]{:S(2)}) collective-permute-start(bf16[64,512]{1,0:T(8,128)(2,1)S(1)} %get-tuple-element.16), channel_id=1, source_target_pairs={{0,2},{2,4},{4,6},{6,8},{8,10},{10,12},{12,14},{14,16},{16,18},{18... | collective-permute-start | bytes 196616 | tf_op jit(solution)/shard_map/ppermute | solution.py:11
  28.5 1.0 copy-start.5
  29.5 0.9 copy-start.6
  29.5 0.9 copy-start.7
  30.9 1.1 copy-start
  32.0 1.5 copy-start.3
  42.3 18.3 %collective-permute-start.7 = (bf16[64,512]{1,0:T(8,128)(2,1)S(1)}, bf16[64,512]{1,0:T(8,128)(2,1)}, u32[]{:S(2)}, u32[]{:S(2)}) collective-permute-start(bf16[64,512]{1,0:T(8,128)(2,1)S(1)} %get-tuple-element.13), channel_id=1, source_target_pairs={{0,1},{2,3},{4,5},{6,7},{8,9},{10,11},{12,13},{14,15},{16,17},{18,... | collective-permute-start | bytes 196616 | tf_op jit(solution)/shard_map/ppermute | solution.py:17
  44.2 16.4 %collective-permute-start.6 = (bf16[64,512]{1,0:T(8,128)(2,1)S(1)}, bf16[64,512]{1,0:T(8,128)(2,1)}, u32[]{:S(2)}, u32[]{:S(2)}) collective-permute-start(bf16[64,512]{1,0:T(8,128)(2,1)S(1)} %get-tuple-element.14), channel_id=1, source_target_pairs={{1,0},{3,2},{5,4},{7,6},{9,8},{11,10},{13,12},{15,14},{17,16},{19,... | collective-permute-start | bytes 196616 | tf_op jit(solution)/shard_map/ppermute | solution.py:17
  45.5 15.1 %collective-permute-start.5 = (bf16[64,512]{1,0:T(8,128)(2,1)S(1)}, bf16[64,512]{1,0:T(8,128)(2,1)}, u32[]{:S(2)}, u32[]{:S(2)}) collective-permute-start(bf16[64,512]{1,0:T(8,128)(2,1)S(1)} %get-tuple-element.15), channel_id=1, source_target_pairs={{0,2},{2,4},{4,6},{6,8},{8,10},{10,12},{12,14},{14,16},{16,18},{18... | collective-permute-start | bytes 196616 | tf_op jit(solution)/shard_map/ppermute | solution.py:11
  45.5 15.0 %collective-permute-start.4 = (bf16[64,512]{1,0:T(8,128)(2,1)S(1)}, bf16[64,512]{1,0:T(8,128)(2,1)}, u32[]{:S(2)}, u32[]{:S(2)}) collective-permute-start(bf16[64,512]{1,0:T(8,128)(2,1)S(1)} %get-tuple-element.12), channel_id=1, source_target_pairs={{0,30},{2,0},{4,2},{6,4},{8,6},{10,8},{12,10},{14,12},{16,14},{18,... | collective-permute-start | bytes 196616 | tf_op jit(solution)/shard_map/ppermute | solution.py:11
  53.7 6.9 %copy-start.9 = (s32[1,4,64]{2,1,0:T(4,128)S(1)}, s32[1,4,64]{2,1,0:T(4,128)}, u32[]{:S(2)}) copy-start(s32[1,4,64]{2,1,0:T(4,128)} %param.19) | copy-start | bytes 3076
  178.3 3.5 %copy-start.2 = (f32[512,512]{1,0:T(8,128)S(1)}, f32[512,512]{1,0:T(8,128)}, u32[]{:S(2)}) copy-start(f32[512,512]{1,0:T(8,128)} %get-tuple-element.11) | copy-start | bytes 3145732
Sparse Core Ops, SparseCore 0:
  36.3 141.9 all-reduce.2
where the time goes:
time: 193 us; the launch traced here: 192 us
  waiting for transfers between devices  119 us (62%)
  starting transfers between devices  20.2 us (10%)
  matrix products  18.9 us (10%)
  between operations  15.6 us (8%)
  other arithmetic  11.6 us (6%)
  local copies, waits for them, and re-layouts  7.15 us (4%)
    psum x1, waiting for transfers between devices, per_device(): lax.psum((first_grad, second_grad), ('wide', 'narrow'))  116 us
    ppermute x4, starting transfers between devices, shifted(): return lax.ppermute(value, axis, pairs)  12.7 us
    ppermute x4, starting transfers between devices, shifted_2(): return lax.ppermute(block, axis, route)  7.52 us
    unnamed x23, local copies, waits for them, and re-layouts  6.07 us
    dot_general x2, matrix products, edge_contract(): lax.dot_general(hot_table, values, (((0,), (0,)), ((), ())), precision=la...  4.11 us
  transfers between devices with their start and end apart: 9, of which 2 were waited for; matrix products, arithmetic and copies ran while one was open for 12% of the time, Pallas kernels for 0%

commit v1 on v0

--- a/solution.py
+++ b/solution.py
@@ -138,7 +138,9 @@
     second_rows = w_second.shape[0] // wide_count
     first_weight_sq = jnp.sum(jnp.square(w_first.astype(jnp.float32)), 0)
     second_weight_sq = jnp.sum(jnp.square(w_second.astype(jnp.float32)), 0)
-    first_total, second_total = lax.psum((first_grad, second_grad), ("wide", "narrow"))
+    first_total, second_total = lax.psum(
+        lax.psum((first_grad, second_grad), axis_name="narrow"), "wide"
+    )
     position = lax.axis_index("wide")
     first_share = lax.dynamic_slice_in_dim(first_total, position * first_rows, first_rows, 0)
     second_share = lax.dynamic_slice_in_dim(second_total, position * second_rows, second_rows, 0)

time: 193 us -> 254 us (1.32)
  waiting for transfers between devices: 119 us -> 179 us
    psum x1 -> x2, waiting for transfers between devices: 116 us -> 176 us  [the longest x1 149 us: per_device(): lax.psum(lax.psum((first_grad, second_grad), axis_name='narrow'), 'wide')]
  transfers between devices with their start and end apart: 9 -> 10, of which waited for: 2 -> 3; matrix products, arithmetic and copies ran while one was open for 12% -> 9% of each run, Pallas kernels for 0% -> 0%
where the time goes in v1:
time: 254 us
  waiting for transfers between devices  179 us (70%)
  starting transfers between devices  21.1 us (8%)
  matrix products  18.9 us (7%)
  between operations  15.6 us (6%)
  other arithmetic  11.5 us (5%)
  local copies, waits for them, and re-layouts  7.14 us (3%)
    psum x1, waiting for transfers between devices, per_device(): lax.psum(lax.psum((first_grad, second_grad), axis_name='narrow'), 'wide')  149 us
    psum x1, waiting for transfers between devices, per_device(): lax.psum((first_grad, second_grad), axis_name='narrow')  26.6 us
    ppermute x4, starting transfers between devices, shifted(): return lax.ppermute(value, axis, pairs)  12.7 us
    ppermute x4, starting transfers between devices, shifted_2(): return lax.ppermute(block, axis, route)  8.36 us
    unnamed x23, local copies, waits for them, and re-layouts  6.06 us
  transfers between devices with their start and end apart: 10, of which 3 were waited for; matrix products, arithmetic and copies ran while one was open for 9% of the time, Pallas kernels for 0%

profile of v1, /device:TPU:0, one launch (start us, length us, event | category | flops | bytes accessed | tf_op | source)
XLA Modules:
  0.0 253.6 jit_solution(11567867524157199663)
XLA Ops:
  7.2 0.0 copy-start.4
  7.2 0.0 copy-start.8
  7.2 0.0 copy-start.1
  7.2 0.0 all-reduce.7.cloned.1.call-start
  7.2 1.3 convolution_convert_fusion.2
  8.6 1.3 collective-permute-start.3
  9.9 3.0 %collective-permute-start.2 = (bf16[64,512]{1,0:T(8,128)(2,1)S(1)}, bf16[64,512]{1,0:T(8,128)(2,1)S(1)}, u32[]{:S(2)}, u32[]{:S(2)}) collective-permute-start(bf16[64,512]{1,0:T(8,128)(2,1)S(1)} %get-tuple-element.20), channel_id=1, source_target_pairs={{0,1},{2,3},{4,5},{6,7},{8,9},{10,11},{12,13},{14,15},{16,17},{18,... | collective-permute-start | bytes 196616 | tf_op jit(solution)/shard_map/ppermute | solution.py:17
  12.9 7.0 %collective-permute-start.1 = (bf16[64,512]{1,0:T(8,128)(2,1)S(1)}, bf16[64,512]{1,0:T(8,128)(2,1)S(1)}, u32[]{:S(2)}, u32[]{:S(2)}) collective-permute-start(bf16[64,512]{1,0:T(8,128)(2,1)S(1)} %get-tuple-element.21), channel_id=1, source_target_pairs={{0,30},{2,0},{4,2},{6,4},{8,6},{10,8},{12,10},{14,12},{16,14},{18,... | collective-permute-start | bytes 196616 | tf_op jit(solution)/shard_map/ppermute | solution.py:11
  19.9 0.0 collective-permute-start
  19.9 1.3 convolution_convert_fusion.1
  21.3 0.7 convert_element_type.56
  22.0 0.7 convert_element_type.55
  22.6 1.3 copy.15
  23.9 0.7 convert_element_type.53
  24.6 0.0 collective-permute-done.3
  24.6 0.0 collective-permute-done.2
  24.6 0.0 collective-permute-done.1
  24.6 3.2 %collective-permute-done = bf16[64,512]{1,0:T(8,128)(2,1)S(1)} collective-permute-done((bf16[64,512]{1,0:T(8,128)(2,1)S(1)}, bf16[64,512]{1,0:T(8,128)(2,1)S(1)}, u32[]{:S(2)}, u32[]{:S(2)}) %collective-permute-start) | collective-permute-done | bytes 65568 | tf_op jit(solution)/shard_map/ppermute | solution.py:11
  27.8 0.0 copy-done.4
  27.8 0.0 copy-done.8
  27.9 0.6 convolution_convert_fusion
  28.5 0.0 copy-done.1
  28.5 0.0 copy-start.5
  28.5 1.0 convolution_add_fusion.1
  29.5 0.0 copy-done.5
  29.5 0.6 fusion.33
  30.2 0.2 multiply_reduce_fusion.5
  30.4 0.1 copy-done.6
  30.4 0.5 multiply_reduce_fusion.6
  31.0 0.3 multiply_convert_fusion
  31.3 0.7 fusion.1
  31.9 0.1 copy-done
  32.0 1.5 fusion.31
  33.5 2.7 %fusion.7 = f32[1536,512]{1,0:T(8,128)} fusion(bf16[512,512]{1,0:T(8,128)(2,1)S(1)} %fusion.1, bf16[512,512]{0,1:T(8,128)(2,1)S(1)} %convolution_convert_fusion.1, bf16[512,512]{0,1:T(8,128)(2,1)S(1)} %convolution_convert_fusion, bf16[512,512]{0,1:T(8,128)(2,1)S(1)} %copy.15), kind=kOutput, calls=%fused_computation.28 | convolution fusion | flops 810024960 | bytes 5242880 | tf_op jit(solution)/shard_map/dot_general | solution.py:119
  36.2 0.0 all-reduce.7.cloned.1.call-update
  36.2 0.0 all-reduce.5.cloned.1.call-start
  36.2 26.6 %all-reduce.7.cloned.1.call-done = (f32[1536,512]{1,0:T(8,128)}, f32[512,512]{1,0:T(8,128)}) async-done(((f32[1536,512]{1,0:T(8,128)}, f32[512,512]{1,0:T(8,128)}), (f32[1536,512]{1,0:T(8,128)}, f32[512,512]{1,0:T(8,128)})) %all-reduce.7.cloned.1.call-update) | async-done | bytes 4194320 | tf_op jit(solution)/shard_map/psum | solution.py:142
  62.9 0.0 all-reduce.5.cloned.1.call-update
  62.9 0.2 multiply_reduce_fusion.2
  63.1 0.4 multiply_reduce_fusion
  63.5 2.6 %fusion.35 = f32[512,1536]{1,0:T(8,128)S(1)} fusion(bf16[512,512]{1,0:T(8,128)(2,1)} %copy-done.3, bf16[1536,512]{1,0:T(8,128)(2,1)} %param.14), kind=kOutput, calls=%fused_computation.74 | convolution fusion | flops 805306368 | bytes 5242880 | tf_op jit(solution)/shard_map/dot_general | solution.py:122
  66.1 1.0 slice.69
  67.1 1.9 fusion.34
  69.0 2.8 %collective-permute-start.7 = (bf16[64,512]{1,0:T(8,128)(2,1)S(1)}, bf16[64,512]{1,0:T(8,128)(2,1)}, u32[]{:S(2)}, u32[]{:S(2)}) collective-permute-start(bf16[64,512]{1,0:T(8,128)(2,1)S(1)} %get-tuple-element.15), channel_id=1, source_target_pairs={{0,1},{2,3},{4,5},{6,7},{8,9},{10,11},{12,13},{14,15},{16,17},{18,... | collective-permute-start | bytes 196616 | tf_op jit(solution)/shard_map/ppermute | solution.py:17
  71.7 1.3 collective-permute-start.6
  73.0 1.9 collective-permute-start.5
  74.9 3.8 %collective-permute-start.4 = (bf16[64,512]{1,0:T(8,128)(2,1)S(1)}, bf16[64,512]{1,0:T(8,128)(2,1)}, u32[]{:S(2)}, u32[]{:S(2)}) collective-permute-start(bf16[64,512]{1,0:T(8,128)(2,1)S(1)} %get-tuple-element.14), channel_id=1, source_target_pairs={{0,30},{2,0},{4,2},{6,4},{8,6},{10,8},{12,10},{14,12},{16,14},{18,... | collective-permute-start | bytes 196616 | tf_op jit(solution)/shard_map/ppermute | solution.py:11
  78.7 2.5 %copy.18 = f32[512,512]{0,1:T(8,128)} copy(f32[512,512]{1,0:T(8,128)} %slice.69) | data formatting | bytes 2097152
  81.2 2.5 add_convert_fusion
  83.7 2.3 convolution_add_fusion.2
  86.0 2.0 copy.17
  88.0 0.0 collective-permute-done.7
  88.0 0.0 collective-permute-done.6
  88.1 0.0 collective-permute-done.5
  88.1 0.0 collective-permute-done.4
  88.1 2.0 fusion.3
  90.1 149.4 %all-reduce.5.cloned.1.call-done = (f32[1536,512]{1,0:T(8,128)}, f32[512,512]{1,0:T(8,128)}) async-done(((f32[1536,512]{1,0:T(8,128)}, f32[512,512]{1,0:T(8,128)}), (f32[1536,512]{1,0:T(8,128)}, f32[512,512]{1,0:T(8,128)})) %all-reduce.5.cloned.1.call-update) | async-done | bytes 4194320 | tf_op jit(solution)/shard_map/psum | solution.py:141
  239.5 2.3 multiply_reduce_fusion.1
  241.7 0.6 sqrt_reduce_fusion.1
  243.0 0.0 copy-done.2
  243.0 0.1 multiply_reduce_fusion.3
  243.2 0.6 sqrt_reduce_fusion
  244.4 1.6 multiply_multiply_fusion
  246.1 0.6 multiply_multiply_fusion.1
  (17 shorter events, 0.1 us)
Async XLA Ops:
  7.2 20.7 %copy-start.4 = (bf16[128,512]{1,0:T(8,128)(2,1)S(1)}, bf16[128,512]{1,0:T(8,128)(2,1)}, u32[]{:S(2)}) copy-start(bf16[128,512]{1,0:T(8,128)(2,1)} %param.11) | copy-start | bytes 393220
  7.2 20.7 %copy-start.8 = (s32[512]{0:T(512)S(1)}, s32[512]{0:T(512)}, u32[]{:S(2)}) copy-start(s32[512]{0:T(512)} %param.20) | copy-start | bytes 6148
  7.2 21.3 %copy-start.1 = (bf16[1536,512]{1,0:T(8,128)(2,1)S(1)}, bf16[1536,512]{1,0:T(8,128)(2,1)}, u32[]{:S(2)}) copy-start(bf16[1536,512]{1,0:T(8,128)(2,1)} %param.14) | copy-start | bytes 4718596
  7.2 55.7 %all-reduce.7.cloned.1.call-start = ((), (), s32[]{:S(2)}) async-start(), calls=%async_computation.1 | async-start | bytes 8388608 | tf_op jit(solution)/shard_map/psum | solution.py:142
  8.6 16.0 %collective-permute-start.3 = (bf16[64,512]{1,0:T(8,128)(2,1)S(1)}, bf16[64,512]{1,0:T(8,128)(2,1)S(1)}, u32[]{:S(2)}, u32[]{:S(2)}) collective-permute-start(bf16[64,512]{1,0:T(8,128)(2,1)S(1)} %get-tuple-element.19), channel_id=1, source_target_pairs={{1,0},{3,2},{5,4},{7,6},{9,8},{11,10},{13,12},{15,14},{17,16},{19,... | collective-permute-start | bytes 196616 | tf_op jit(solution)/shard_map/ppermute | solution.py:17
  9.9 14.7 %collective-permute-start.2 = (bf16[64,512]{1,0:T(8,128)(2,1)S(1)}, bf16[64,512]{1,0:T(8,128)(2,1)S(1)}, u32[]{:S(2)}, u32[]{:S(2)}) collective-permute-start(bf16[64,512]{1,0:T(8,128)(2,1)S(1)} %get-tuple-element.20), channel_id=1, source_target_pairs={{0,1},{2,3},{4,5},{6,7},{8,9},{10,11},{12,13},{14,15},{16,17},{18,... | collective-permute-start | bytes 196616 | tf_op jit(solution)/shard_map/ppermute | solution.py:17
  12.9 11.7 %collective-permute-start.1 = (bf16[64,512]{1,0:T(8,128)(2,1)S(1)}, bf16[64,512]{1,0:T(8,128)(2,1)S(1)}, u32[]{:S(2)}, u32[]{:S(2)}) collective-permute-start(bf16[64,512]{1,0:T(8,128)(2,1)S(1)} %get-tuple-element.21), channel_id=1, source_target_pairs={{0,30},{2,0},{4,2},{6,4},{8,6},{10,8},{12,10},{14,12},{16,14},{18,... | collective-permute-start | bytes 196616 | tf_op jit(solution)/shard_map/ppermute | solution.py:11
  19.9 7.9 %collective-permute-start = (bf16[64,512]{1,0:T(8,128)(2,1)S(1)}, bf16[64,512]{1,0:T(8,128)(2,1)S(1)}, u32[]{:S(2)}, u32[]{:S(2)}) collective-permute-start(bf16[64,512]{1,0:T(8,128)(2,1)S(1)} %get-tuple-element.18), channel_id=1, source_target_pairs={{0,2},{2,4},{4,6},{6,8},{8,10},{10,12},{12,14},{14,16},{16,18},{18... | collective-permute-start | bytes 196616 | tf_op jit(solution)/shard_map/ppermute | solution.py:11
  28.5 1.0 copy-start.5
  29.5 0.9 copy-start.6
  29.5 0.9 copy-start.7
  30.9 1.1 copy-start
  32.0 1.5 copy-start.3
  36.2 203.3 %all-reduce.5.cloned.1.call-start = ((), (), s32[]{:S(2)}) async-start(), calls=%async_computation | async-start | bytes 8388608 | tf_op jit(solution)/shard_map/psum | solution.py:141
  69.0 19.1 %collective-permute-start.7 = (bf16[64,512]{1,0:T(8,128)(2,1)S(1)}, bf16[64,512]{1,0:T(8,128)(2,1)}, u32[]{:S(2)}, u32[]{:S(2)}) collective-permute-start(bf16[64,512]{1,0:T(8,128)(2,1)S(1)} %get-tuple-element.15), channel_id=1, source_target_pairs={{0,1},{2,3},{4,5},{6,7},{8,9},{10,11},{12,13},{14,15},{16,17},{18,... | collective-permute-start | bytes 196616 | tf_op jit(solution)/shard_map/ppermute | solution.py:17
  71.7 16.3 %collective-permute-start.6 = (bf16[64,512]{1,0:T(8,128)(2,1)S(1)}, bf16[64,512]{1,0:T(8,128)(2,1)}, u32[]{:S(2)}, u32[]{:S(2)}) collective-permute-start(bf16[64,512]{1,0:T(8,128)(2,1)S(1)} %get-tuple-element.16), channel_id=1, source_target_pairs={{1,0},{3,2},{5,4},{7,6},{9,8},{11,10},{13,12},{15,14},{17,16},{19,... | collective-permute-start | bytes 196616 | tf_op jit(solution)/shard_map/ppermute | solution.py:17
  73.0 15.0 %collective-permute-start.5 = (bf16[64,512]{1,0:T(8,128)(2,1)S(1)}, bf16[64,512]{1,0:T(8,128)(2,1)}, u32[]{:S(2)}, u32[]{:S(2)}) collective-permute-start(bf16[64,512]{1,0:T(8,128)(2,1)S(1)} %get-tuple-element.17), channel_id=1, source_target_pairs={{0,2},{2,4},{4,6},{6,8},{8,10},{10,12},{12,14},{14,16},{16,18},{18... | collective-permute-start | bytes 196616 | tf_op jit(solution)/shard_map/ppermute | solution.py:11
  74.9 13.2 %collective-permute-start.4 = (bf16[64,512]{1,0:T(8,128)(2,1)S(1)}, bf16[64,512]{1,0:T(8,128)(2,1)}, u32[]{:S(2)}, u32[]{:S(2)}) collective-permute-start(bf16[64,512]{1,0:T(8,128)(2,1)S(1)} %get-tuple-element.14), channel_id=1, source_target_pairs={{0,30},{2,0},{4,2},{6,4},{8,6},{10,8},{12,10},{14,12},{16,14},{18,... | collective-permute-start | bytes 196616 | tf_op jit(solution)/shard_map/ppermute | solution.py:11
  81.2 6.8 %copy-start.9 = (s32[1,4,64]{2,1,0:T(4,128)S(1)}, s32[1,4,64]{2,1,0:T(4,128)}, u32[]{:S(2)}) copy-start(s32[1,4,64]{2,1,0:T(4,128)} %param.19) | copy-start | bytes 3076
  239.5 3.5 %copy-start.2 = (f32[512,512]{1,0:T(8,128)S(1)}, f32[512,512]{1,0:T(8,128)}, u32[]{:S(2)}) copy-start(f32[512,512]{1,0:T(8,128)} %get-tuple-element.11) | copy-start | bytes 3145732
Sparse Core Ops, SparseCore 0:
  36.3 26.5 all-reduce.6
  68.6 170.8 all-reduce.4
